TPU v7x, 16 devices: a whole 2x2x2 slice. The times are simulated.
16 devices in a mesh: dp: 4 (over z, y), cp: 4 (over x, core).
Axes of the slice: x: 2, y: 2, z: 2, core: 2. Of those that a mesh axis runs over, the one named last changes fastest.
Arguments:
- hidden_in: bfloat16 [128, 768, 384], P('dp', 'cp'), parts along dimension 0
- pad_mask: int32 [128, 768], P('dp', 'cp'), parts along dimension 0
- d_out: bfloat16 [128, 768, 384], P('dp', 'cp'), parts along dimension 0
- g_attn: bfloat16 [2, 384], replicated
- g_mlp: bfloat16 [2, 384], replicated
- w_qkv: bfloat16 [2, 384, 1152], replicated
- w_out: bfloat16 [2, 384, 384], replicated
- w_in: bfloat16 [2, 384, 1152], replicated
- w_down: bfloat16 [2, 576, 384], replicated
Outputs:
- output 1: bfloat16 [128, 768, 384], P('dp', 'cp'), parts along dimension 0
- output 2: bfloat16 [128, 768, 384], P('dp', 'cp'), parts along dimension 0
- output 3: float32 [8, 384], P('dp'), parts along dimension 0
- output 4: float32 [8, 384], P('dp'), parts along dimension 0
- output 5: float32 [8, 384, 1152], P('dp'), parts along dimension 0
- output 6: float32 [8, 384, 384], P('dp'), parts along dimension 0
- output 7: float32 [8, 384, 1152], P('dp'), parts along dimension 0
- output 8: float32 [8, 576, 384], P('dp'), parts along dimension 0
There are 4 independent parts. A program takes and returns all parts, laid end to end along the dimension named above; an argument that names none is the same for every part.
All inputs are finite; a program needn't handle non-finite values.
Results may differ from a plain program's by a relative error of at most 0.02.
Values are sent between devices in bfloat16 or wider.
A program may use at most 1 GiB of HBM per device.

v0:
```python
import numpy as np
import jax
import jax.numpy as jnp
from jax import lax
from jax.experimental import pallas as pl
from jax.experimental.pallas import tpu as pltpu
from jax.sharding import PartitionSpec as P

HEADS = 6
HD = 64
WIN = 64
EPS = 1e-5
THETAS = (10000.0, 160000.0)
NEG = -1e30
SEQ = 768
DIM = 384
FFN = 576
CH = 256
NCH = SEQ // CH
F32 = jnp.float32
BF16 = jnp.bfloat16
KEYS = (((0, 384), (128, 640), (384, 768)), ((0, 768),) * 3)


def rope_tables():
    out = np.zeros((2, 2, HD // 2, SEQ), np.float32)
    pos = np.arange(SEQ, dtype=np.float32)
    for l, theta in enumerate(THETAS):
        freq = np.float32(theta) ** (-np.arange(0, HD, 2, dtype=np.float32) / np.float32(HD))
        ang = (pos[None, :] * freq.astype(np.float32)[:, None]).astype(np.float32).astype(np.float64)
        out[l, 0] = np.cos(ang)
        out[l, 1] = np.sin(ang)
    return out


def nn(a, b):
    return jnp.dot(a, b, preferred_element_type=F32)


def nt(a, b):
    return lax.dot_general(a, b, (((1,), (1,)), ((), ())), preferred_element_type=F32)


def wide(g):
    return jnp.concatenate([g] * (CH // 128), axis=1)


def fold(z):
    return sum(z[:, i * 128:(i + 1) * 128] for i in range(1, CH // 128)) + z[:, :128]


def ln_fwd(z, gain, st, row, sl):
    mean = jnp.sum(z, axis=0, keepdims=True) * (1.0 / DIM)
    c = z - mean
    var = jnp.sum(c * c, axis=0, keepdims=True) * (1.0 / DIM)
    r = lax.rsqrt(var + EPS)
    st[row:row + 1, sl] = mean
    st[row + 1:row + 2, sl] = r
    return (c * r * wide(gain)).astype(BF16)


def ln_bwd(z, du, gain, st, row, sl):
    mean = st[row:row + 1, sl]
    r = st[row + 1:row + 2, sl]
    xhat = (z - mean) * r
    dg = fold(du * xhat)
    gw = wide(gain)
    dxh = du * gw
    m1 = jnp.sum(dxh, axis=0, keepdims=True) * (1.0 / DIM)
    m2 = jnp.sum(dxh * xhat, axis=0, keepdims=True) * (1.0 / DIM)
    return r * (dxh - m1 - xhat * m2), dg, (xhat * gw).astype(BF16)


def turn(z, cos, sin):
    n = z.shape[0] // HD
    z4 = z.reshape(n, 2, HD // 2, z.shape[1])
    a, b = z4[:, 0], z4[:, 1]
    return jnp.stack([a * cos - b * sin, b * cos + a * sin], axis=1).reshape(z.shape)


def gelu_parts(a):
    cdf = 0.5 * (1.0 + lax.erf(a * (2.0 ** -0.5)))
    return a * cdf, cdf


class Bufs:
    pass


def forward(l, b, write_y):
    st = b.st.at[l]
    for c in range(NCH):
        sl = pl.ds(c * CH, CH)
        u = ln_fwd(b.xT[l, :, sl].astype(F32), b.g[0, l], st, 0, sl)
        z = nn(b.wTqkv[l], u)
        cos, sin = b.rope[l, 0, :, sl], b.rope[l, 1, :, sl]
        b.qkvT[l, :DIM, sl] = turn(z[:DIM], cos * 0.125, sin * 0.125).astype(BF16)
        b.qkvT[l, DIM:2 * DIM, sl] = turn(z[DIM:2 * DIM], cos, sin).astype(BF16)
        b.qkvT[l, 2 * DIM:, sl] = z[2 * DIM:].astype(BF16)

    def head(h):
        row = pl.multiple_of(h * HD, HD)
        kT = b.qkvT[l, pl.ds(DIM + row, HD), :]
        vT = b.qkvT[l, pl.ds(2 * DIM + row, HD), :]
        if l == 0:
            kn = kT.T
        else:
            kn = jnp.concatenate([kT, b.kextra[...]], axis=0).T
        for c in range(NCH):
            sl = pl.ds(c * CH, CH)
            k0, k1 = KEYS[l][c]
            qT = b.qkvT[l, pl.ds(row, HD), sl]
            if l == 0:
                s = nn(kn[k0:k1], qT) + b.bias[c, :k1 - k0, :].astype(F32)
            else:
                s = nn(kn, jnp.concatenate([qT, b.qextra[...]], axis=0))
            m = jnp.max(s, axis=0, keepdims=True)
            e = jnp.exp(s - m)
            p = (e * (1.0 / jnp.sum(e, axis=0, keepdims=True))).astype(BF16)
            if l == 0:
                b.p0[h, c, :k1 - k0, :] = p
            else:
                b.p1[h, :, sl] = p
            b.oT[l, pl.ds(row, HD), sl] = nn(vT[:, k0:k1], p).astype(BF16)

    def pair(i, carry):
        head(2 * i)
        head(2 * i + 1)
        return carry
    lax.fori_loop(0, HEADS // 2, pair, 0)

    for c in range(NCH):
        sl = pl.ds(c * CH, CH)
        hb = (b.xT[l, :, sl].astype(F32) + nn(b.wTout[l], b.oT[l, :, sl])).astype(BF16)
        b.hT[l, :, sl] = hb
        u2 = ln_fwd(hb.astype(F32), b.g[1, l], st, 2, sl)
        mix = nn(b.wTin[l], u2)
        b.mixT[l, :, sl] = mix
        act = (gelu_parts(mix[:FFN])[0] * mix[FFN:]).astype(BF16)
        y = (hb.astype(F32) + nn(b.wTdown[l], act)).astype(BF16)
        write_y(c, sl, y)


def backward(l, b, read_dy, write_dx):
    st = b.st.at[l]
    for c in range(NCH):
        sl = pl.ds(c * CH, CH)
        dy = read_dy(c, sl)
        dyb = dy.astype(BF16)
        b.dybT[:, sl] = dyb
        dact = nn(b.wdown[l], dyb)
        a, g = b.mixT[l, :FFN, sl], b.mixT[l, FFN:, sl]
        ge, cdf = gelu_parts(a)
        b.actT[:, sl] = (ge * g).astype(BF16)
        pdf = jnp.exp(a * a * -0.5) * 0.3989422804014327
        b.dbigT[:FFN, sl] = (dact * g * (cdf + a * pdf)).astype(BF16)
        b.dbigT[FFN:, sl] = (dact * ge).astype(BF16)
        du = nn(b.win[l], b.dbigT[:, sl])
        dn, dg, b.uT[:, sl] = ln_bwd(b.hT[l, :, sl].astype(F32), du, b.g[1, l], st, 2, sl)
        b.dg[1, l] += dg
        dh = dy + dn
        b.dyT[:, sl] = dh
        dhb = dh.astype(BF16)
        b.dhbT[:, sl] = dhb
        b.doT[:, sl] = nn(b.wout[l], dhb).astype(BF16)
    b.adown[l] += nt(b.actT[...], b.dybT[...])
    b.ain[l] += nt(b.uT[...], b.dbigT[...])
    b.aout[l] += nt(b.oT[l], b.dhbT[...])

    def head(h):
        row = pl.multiple_of(h * HD, HD)
        qT = b.qkvT[l, pl.ds(row, HD), :]
        kT = b.qkvT[l, pl.ds(DIM + row, HD), :]
        vn = b.qkvT[l, pl.ds(2 * DIM + row, HD), :].T
        doT = b.doT[pl.ds(row, HD), :]
        prod = doT.astype(F32) * b.oT[l, pl.ds(row, HD), :].astype(F32)
        delta = jnp.sum(prod, axis=0, keepdims=True)
        dq, dk, dv = [], [None] * 6, [None] * 6
        if l == 1:
            dvT = nt(doT, b.p1[h])
        for c in range(NCH):
            cs = slice(c * CH, (c + 1) * CH)
            sl = pl.ds(c * CH, CH)
            k0, k1 = KEYS[l][c]
            p = b.p0[h, c, :k1 - k0, :] if l == 0 else b.p1[h, :, sl]
            dp = nn(vn[k0:k1], doT[:, cs])
            ds = (p.astype(F32) * (dp - delta[:, cs])).astype(BF16)
            dq.append(nn(kT[:, k0:k1], ds) * 0.125)
            if l == 1:
                b.p1[h, :, sl] = ds
            else:
                dkc, dvc = nt(qT[:, cs], ds), nt(doT[:, cs], p)
                for j in range(k0 // 128, k1 // 128):
                    js = slice(j * 128 - k0, (j + 1) * 128 - k0)
                    dk[j] = dkc[:, js] if dk[j] is None else dk[j] + dkc[:, js]
                    dv[j] = dvc[:, js] if dv[j] is None else dv[j] + dvc[:, js]
        if l == 1:
            dkT = nt(qT, b.p1[h])
        else:
            dkT, dvT = jnp.concatenate(dk, axis=1), jnp.concatenate(dv, axis=1)
        dqT = jnp.concatenate(dq, axis=1)
        cos, sin = b.rope[l, 0], -b.rope[l, 1]
        b.dbigT[pl.ds(row, HD), :] = turn(dqT, cos, sin).astype(BF16)
        b.dbigT[pl.ds(DIM + row, HD), :] = turn(dkT, cos, sin).astype(BF16)
        b.dbigT[pl.ds(2 * DIM + row, HD), :] = dvT.astype(BF16)

    def pair(i, carry):
        head(2 * i)
        head(2 * i + 1)
        return carry
    lax.fori_loop(0, HEADS // 2, pair, 0)

    for c in range(NCH):
        sl = pl.ds(c * CH, CH)
        du = nn(b.wqkv[l], b.dbigT[:, sl])
        dn, dg, b.uT[:, sl] = ln_bwd(b.xT[l, :, sl].astype(F32), du, b.g[0, l], st, 0, sl)
        b.dg[0, l] += dg
        write_dx(c, sl, b.dyT[:, sl] + dn)
    b.aqkv[l] += nt(b.uT[...], b.dbigT[...])


def start_up(b):
    for src, dst in ((b.wqkv, b.wTqkv), (b.wout, b.wTout), (b.win, b.wTin), (b.wdown, b.wTdown)):
        for l in range(2):
            dst[l] = src[l].T
    for acc in (b.aqkv, b.aout, b.ain, b.adown, b.dg):
        acc[...] = jnp.zeros_like(acc)
    row0 = lax.broadcasted_iota(jnp.int32, (HD, CH), 0) == 0
    b.qextra[...] = jnp.where(row0, 1.0, 0.0).astype(BF16)


def masks(b, pad):
    ok = pad > 0
    row0 = lax.broadcasted_iota(jnp.int32, (HD, SEQ), 0) == 0
    b.kextra[...] = jnp.where(row0 & jnp.logical_not(ok), NEG, 0.0).astype(BF16)
    okc = jnp.broadcast_to(jnp.where(ok, 1.0, 0.0), (128, SEQ)).T
    for c in range(NCH):
        k0, k1 = KEYS[0][c]
        shape = (k1 - k0, CH)
        off = lax.broadcasted_iota(jnp.int32, shape, 0) + (k0 - c * CH) - lax.broadcasted_iota(jnp.int32, shape, 1)
        near = (jnp.abs(off) <= WIN) & (wide(okc[k0:k1]) > 0.5)
        b.bias[c, :k1 - k0, :] = jnp.where(near | (off == 0), 0.0, NEG).astype(BF16)


NAMES = ('wTqkv', 'wTout', 'wTin', 'wTdown', 'aqkv', 'aout', 'ain', 'adown', 'dg', 'st', 'xT', 'uT', 'qkvT',
         'p0', 'p1', 'oT', 'hT', 'mixT', 'actT', 'dyT', 'dybT', 'dbigT', 'dhbT', 'doT', 'bias',
         'kextra', 'qextra', 'xbuf', 'dbuf', 'ybuf', 'dxbuf', 'padin', 'padrow', 'dgs', 'dgl', 'dgb', 'dgr',
         'in_send', 'in_recv', 'pad_send', 'pad_recv', 'fetch', 'out_send', 'out_recv', 'own', 'ready',
         'g_send', 'g_recv', 'g_own')

N_CP = 4
PER = 8
PIECE = SEQ // N_CP
GROUPS = ((0, 1), (1, 1), (2, 2), (4, 4))
ISSUE = (0, 0, 1, 2)
BLOCKS = tuple([('aqkv', 0, DIM, i * DIM) for i in range(3)] + [('ain', 0, DIM, i * DIM) for i in range(3)]
               + [('aout', 0, DIM, 0), ('adown', 0, DIM, 0), ('adown', DIM, FFN - DIM, 0)])


def scratch():
    v = pltpu.VMEM
    dma, reg = pltpu.SemaphoreType.DMA, pltpu.SemaphoreType.REGULAR
    n_g = len(BLOCKS) + 1
    return [v((2, 3 * DIM, DIM), BF16), v((2, DIM, DIM), BF16), v((2, 2 * FFN, DIM), BF16), v((2, DIM, FFN), BF16),
            v((2, DIM, 3 * DIM), F32), v((2, DIM, DIM), F32), v((2, DIM, 2 * FFN), F32), v((2, FFN, DIM), F32),
            v((2, 2, DIM, 128), F32), v((2, 8, SEQ), F32),
            v((2, DIM, SEQ), BF16), v((DIM, SEQ), BF16), v((2, 3 * DIM, SEQ), BF16),
            v((HEADS, NCH, 512, CH), BF16), v((HEADS, SEQ, SEQ), BF16),
            v((2, DIM, SEQ), BF16), v((2, DIM, SEQ), BF16), v((2, 2 * FFN, SEQ), F32),
            v((FFN, SEQ), BF16), v((DIM, SEQ), F32), v((DIM, SEQ), BF16), v((3 * DIM, SEQ), BF16),
            v((DIM, SEQ), BF16), v((DIM, SEQ), BF16), v((NCH, 512, CH), BF16),
            v((HD, SEQ), BF16), v((HD, CH), BF16),
            v((SEQ, DIM), BF16), v((SEQ, DIM), BF16), v((SEQ, DIM), BF16), v((SEQ, DIM), BF16),
            v((N_CP, PER, PIECE), jnp.int32), v((8, SEQ), jnp.int32),
            v((2, 16, DIM), F32), v((16, DIM), F32), v((16, DIM), BF16), v((16, DIM), BF16),
            dma((2, 3)), dma((2, len(GROUPS), 3)), dma((3,)), dma((3,)), dma((3, N_CP)),
            dma((2, 3)), dma((2, 3)), dma((2,)), reg((2,)),
            dma((3, n_g)), dma((3, n_g)), dma((n_g,))]


def rows(j):
    return pl.ds(pl.multiple_of(j * PIECE, 64), PIECE)


def kernel(x_loc, dout_loc, pad_loc, g_ref, rope_ref, wqkv, wout, win, wdown,
           y_out, dx_out, oqkv, oout, oin, odown, odg, xland, dland, *refs):
    b = Bufs()
    for name, ref in zip(NAMES, refs):
        setattr(b, name, ref)
    b.g, b.rope, b.wqkv, b.wout, b.win, b.wdown = g_ref, rope_ref, wqkv, wout, win, wdown
    me = lax.axis_index('cp')
    core = lax.rem(me, 2)
    mate = me + 1 - 2 * core
    across = lax.rem(me + 2, N_CP)

    def far(d):
        return lax.rem(me + d, N_CP)

    def near(d):
        return lax.rem(me + N_CP - d, N_CP)

    def remote(src, dst, ssem, rsem, j):
        return pltpu.make_async_remote_copy(src_ref=src, dst_ref=dst, send_sem=ssem, recv_sem=rsem,
                                            device_id={'cp': j}, device_id_type=pl.DeviceIdType.MESH)

    ins = ((x_loc, xland), (dout_loc, dland))
    outs = ((b.ybuf, y_out), (b.dxbuf, dx_out))

    def send_in(a, gi, d):
        first, n = GROUPS[gi]
        src, land = ins[a]
        return remote(src.at[pl.ds(far(d) * PER + first, n)], land.at[d - 1, pl.ds(first, n)],
                      b.in_send.at[a, d - 1], b.in_recv.at[a, gi, d - 1], far(d))

    def issue(gi):
        for a in range(2):
            for d in (2, 1, 3):
                send_in(a, gi, d).start()

    def arrived(a, gi):
        for d in (1, 2, 3):
            send_in(a, gi, d).wait_recv()

    def fetches(a, s):
        src, land = ins[a]
        buf = (b.xbuf, b.dbuf)[a]
        res = [pltpu.make_async_copy(src.at[me * PER + s], buf.at[rows(me)], b.fetch.at[a, 0])]
        for d in (1, 2, 3):
            res.append(pltpu.make_async_copy(land.at[d - 1, s], buf.at[rows(near(d))], b.fetch.at[a, d]))
        return res

    def out_copies(a, s):
        buf, out = outs[a]
        res = [remote(buf.at[rows(far(d))], out.at[me * PER + s], b.out_send.at[a, d - 1], b.out_recv.at[a, d - 1], far(d))
               for d in (2, 1, 3)]
        return res, pltpu.make_async_copy(buf.at[rows(me)], out.at[me * PER + s], b.own.at[a])

    def send_out(a, s):
        res, own = out_copies(a, s)
        for c in res:
            c.start()
        own.start()

    def drain_out(a, s):
        res, own = out_copies(a, s)
        for c in res:
            c.wait_send()
        own.wait()

    def pad_copies():
        return [remote(pad_loc.at[pl.ds(pl.multiple_of(far(d) * PER, PER), PER)], b.padin.at[d], b.pad_send.at[d - 1],
                       b.pad_recv.at[d - 1], far(d)) for d in (1, 2, 3)]

    barrier = pltpu.get_barrier_semaphore()
    for d in (1, 2, 3):
        pl.semaphore_signal(barrier, inc=1, device_id={'cp': far(d)}, device_id_type=pl.DeviceIdType.MESH)
    pl.semaphore_wait(barrier, 3)
    for c in pad_copies():
        c.start()
    pad_own = pltpu.make_async_copy(pad_loc.at[pl.ds(pl.multiple_of(me * PER, PER), PER)], b.padin.at[0], b.fetch.at[2, 0])
    pad_own.start()
    for gi in range(len(GROUPS)):
        if ISSUE[gi] == 0:
            issue(gi)
    start_up(b)
    pad_own.wait()
    for c in pad_copies():
        c.wait_recv()
    arrived(0, 0)
    for c in fetches(0, 0):
        c.start()

    def keep(c, sl, y):
        b.xT[1, :, sl] = y

    def put_y(c, sl, y):
        b.ybuf[sl, :] = y.T

    def get_dout(c, sl):
        return b.dbuf[sl, :].T.astype(F32)

    def put_d(c, sl, d):
        b.dyT[:, sl] = d

    def get_d(c, sl):
        return b.dyT[:, sl]

    def put_dx(c, sl, d):
        b.dxbuf[sl, :] = d.astype(BF16).T

    def step(s, carry):
        for gi in range(len(GROUPS)):
            if ISSUE[gi] > 0:
                @pl.when(s == ISSUE[gi])
                def _():
                    issue(gi)
        for j in range(N_CP):
            d = lax.rem(me + N_CP - j, N_CP)
            b.padrow[0:1, j * PIECE:(j + 1) * PIECE] = b.padin[d, pl.ds(s, 1), :]
        masks(b, b.padrow[0:1, :])
        for c in fetches(0, s):
            c.wait()
        b.xT[0] = b.xbuf[...].T
        forward(0, b, keep)
        for gi in range(len(GROUPS)):
            @pl.when(s == GROUPS[gi][0])
            def _():
                arrived(1, gi)
        for c in fetches(1, s):
            c.start()

        @pl.when(s > 0)
        def _():
            drain_out(0, s)
        forward(1, b, put_y)
        send_out(0, s)
        for c in fetches(1, s):
            c.wait()
        backward(1, b, get_dout, put_d)
        for gi in range(1, len(GROUPS)):
            @pl.when(s + 1 == GROUPS[gi][0])
            def _():
                arrived(0, gi)

        @pl.when(s + 1 < PER)
        def _():
            for c in fetches(0, s + 1):
                c.start()

        @pl.when(s > 0)
        def _():
            drain_out(1, s)
        backward(0, b, get_d, put_dx)
        send_out(1, s)
        return carry
    lax.fori_loop(0, PER, step, 0)

    for l in range(2):
        for k in range(2):
            b.dgs[l, k:k + 1, :] = jnp.sum(b.dg[k, l].T, axis=0, keepdims=True)
        b.dgs[l, 2:, :] = jnp.zeros((14, DIM), F32)
    for i, j in enumerate((mate, across)):
        pl.semaphore_signal(b.ready.at[i], inc=1, device_id={'cp': j}, device_id_type=pl.DeviceIdType.MESH)

    grads = {'aqkv': oqkv, 'aout': oout, 'ain': oin, 'adown': odown}

    def tile(ref, i, n):
        return ref.at[i // 6 if ref is b.mixT else i // 4,
                      pl.ds((i % 6 // 2 if ref is b.mixT else i % 4 // 2) * DIM, n), pl.ds(i % 2 * DIM, DIM)]

    def places(i):
        if i == len(BLOCKS):
            return (lambda l: b.dgs.at[l]), b.dgl, b.dgb, b.dgr, (lambda l: odg.at[l])
        name, r0, n, c0 = BLOCKS[i]
        acc, out = getattr(b, name), grads[name]
        return ((lambda l: acc.at[l, pl.ds(r0, n), pl.ds(c0, DIM)]), tile(b.mixT, i, n), tile(b.p1, i, n),
                tile(b.p1, i + 12, n), (lambda l: out.at[l, pl.ds(r0, n), pl.ds(c0, DIM)]))

    n_g = len(BLOCKS) + 1

    def first(i):
        acc, land, _, _, _ = places(i)
        return remote(acc(1 - core), land, b.g_send.at[0, i], b.g_recv.at[0, i], mate)

    def second(i):
        _, _, out, land, _ = places(i)
        return remote(out, land, b.g_send.at[1, i], b.g_recv.at[1, i], across)

    def third(i):
        acc, _, _, _, out = places(i)
        return (remote(acc(core), out(core), b.g_send.at[2, i], b.g_recv.at[2, i], mate),
                pltpu.make_async_copy(acc(core), out(core), b.g_own.at[i]))

    pl.semaphore_wait(b.ready.at[0], 1)
    for i in range(n_g):
        first(i).start()
    pl.semaphore_wait(b.ready.at[1], 1)
    for i in range(n_g):
        acc, land, out, _, _ = places(i)
        first(i).wait_recv()
        out[...] = (acc(core)[...] + land[...]).astype(BF16)
        second(i).start()
    for i in range(n_g):
        acc, _, mine, land, _ = places(i)
        second(i).wait_recv()
        acc(core)[...] = mine[...].astype(F32) + land[...].astype(F32)
        for c in third(i):
            c.start()
    for i in range(n_g):
        first(i).wait_send()
        second(i).wait_send()
        third(i)[0].wait()
        third(i)[1].wait()
    for c in pad_copies():
        c.wait_send()
    for a in range(2):
        drain_out(a, PER - 1)
        src = ins[a][0]
        buf, out = outs[a]
        for d in (1, 2, 3):
            whole_in = src.at[pl.ds(far(d) * PER, PER)]
            remote(whole_in, whole_in, b.in_send.at[a, d - 1], b.in_send.at[a, d - 1], far(d)).wait_send()
            whole_out = out.at[pl.ds(near(d) * PER, PER)]
            remote(whole_out, whole_out, b.out_recv.at[a, d - 1], b.out_recv.at[a, d - 1], near(d)).wait_recv()


def run_kernel(x, dout, pad, g, rope, w_qkv, w_out, w_in, w_down):
    any_spec = pl.BlockSpec(memory_space=pl.ANY)
    vm = pl.BlockSpec(memory_space=pltpu.VMEM)
    sds = jax.ShapeDtypeStruct
    outs = [sds(x.shape, BF16)] * 2 + [
        sds(s, F32) for s in ((2, DIM, 3 * DIM), (2, DIM, DIM), (2, DIM, 2 * FFN), (2, FFN, DIM), (2, 16, DIM))] + [
        sds((3, PER, PIECE, DIM), BF16)] * 2
    return pl.pallas_call(
        kernel, out_shape=outs,
        in_specs=[any_spec] * 3 + [vm] * 6,
        out_specs=[any_spec] * 9,
        scratch_shapes=scratch(),
        compiler_params=pltpu.CompilerParams(vmem_limit_bytes=67043328, collective_id=0, has_side_effects=True),
    )(x, dout, pad, g, rope, w_qkv, w_out, w_in, w_down)


def solution(mesh):
    act_spec = P('dp', 'cp', None)

    def device_pass(x_loc, pad_loc, dout_loc, g_attn, g_mlp, w_qkv, w_out, w_in, w_down):
        g = jnp.broadcast_to(jnp.stack([g_attn, g_mlp]).astype(F32)[..., None], (2, 2, DIM, 128))
        y, dx, dqkv, dout_w, din, ddown, dg = run_kernel(
            x_loc, dout_loc, pad_loc, g, jnp.asarray(rope_tables()), w_qkv, w_out, w_in, w_down)[:7]
        return y, dx, dg[:, 0], dg[:, 1], dqkv, dout_w, din, ddown

    return jax.shard_map(device_pass, mesh=mesh,
                         in_specs=(act_spec, P('dp', 'cp'), act_spec, P(), P(), P(), P(), P(), P()),
                         out_specs=(act_spec, act_spec, P('dp'), P('dp'), P('dp'), P('dp'), P('dp'), P('dp')),
                         check_vma=False)
```

profile of v0, /device:TPU:0, one launch (start us, length us, event | category | flops | bytes accessed | tf_op | source)
XLA Modules:
  0.0 614.1 jit_solution(9550499040991048015)
XLA Ops:
  0.6 0.7 maximum_convert_fusion
  1.3 1.1 broadcast_in_dim.2.g_ref
  2.5 593.3 %shard_map.161 = (bf16[32,192,384]{2,1,0:T(8,128)(2,1)}, bf16[32,192,384]{2,1,0:T(8,128)(2,1)}, f32[2,384,1152]{2,1,0:T(8,128)}, f32[2,384,384]{2,1,0:T(8,128)},...) custom-call(bf16[32,192,384]{2,1,0:T(8,128)(2,1)} %x_loc.1, ...), custom_call_target="tpu_custom_call" | custom-call | tf_op jit(solution)/shard_map/pallas_call | solution.py:514
  595.8 0.8 fusion
  596.6 0.6 copy_bitcast_fusion
  597.2 0.0 copy-start
  597.2 5.2 copy.28
  602.3 0.0 copy-done
  602.3 0.0 copy-start.2
  602.3 2.4 copy.29
  604.7 1.3 copy-done.2
  606.0 0.0 copy-start.4
  606.0 0.0 copy-start.1
  606.0 1.8 copy.30
  607.8 0.3 copy-done.4
  608.1 1.0 copy.31
  609.2 1.0 copy-done.1
  610.1 0.0 copy-start.3
  610.1 1.8 copy.32
  611.9 0.9 copy-done.3
  612.9 1.2 copy.33
Async XLA Ops:
  597.2 5.2 copy-start
  602.3 3.7 copy-start.2
  606.0 2.1 copy-start.4
  606.0 4.1 copy-start.1
  610.1 2.8 copy-start.3
where the time goes:
time: 614 us
  Pallas kernels  593 us (97%)
  local copies, waits for them, and re-layouts  19.4 us (3%)
    pallas_call x1, Pallas kernels, run_kernel(): pl.pallas_call(kernel, out_shape=outs, in_specs=[any_spec] * 3 + [vm] * 6...  593 us
    unnamed x17, local copies, waits for them, and re-layouts  17.5 us

commit v1 on v0

--- a/solution.py
+++ b/solution.py
@@ -89,102 +89,158 @@
 
 def forward(l, b, write_y):
     st = b.st.at[l]
-    for c in range(NCH):
-        sl = pl.ds(c * CH, CH)
-        u = ln_fwd(b.xT[l, :, sl].astype(F32), b.g[0, l], st, 0, sl)
-        z = nn(b.wTqkv[l], u)
+    tmp = {}
+
+    def norm_in(c):
+        sl = pl.ds(c * CH, CH)
+        tmp['z', c] = nn(b.wTqkv[l], ln_fwd(b.xT[l, :, sl].astype(F32), b.g[0, l], st, 0, sl))
+
+    def rotate(c):
+        sl = pl.ds(c * CH, CH)
+        z = tmp.pop(('z', c))
         cos, sin = b.rope[l, 0, :, sl], b.rope[l, 1, :, sl]
         b.qkvT[l, :DIM, sl] = turn(z[:DIM], cos * 0.125, sin * 0.125).astype(BF16)
         b.qkvT[l, DIM:2 * DIM, sl] = turn(z[DIM:2 * DIM], cos, sin).astype(BF16)
         b.qkvT[l, 2 * DIM:, sl] = z[2 * DIM:].astype(BF16)
 
-    def head(h):
-        row = pl.multiple_of(h * HD, HD)
-        kT = b.qkvT[l, pl.ds(DIM + row, HD), :]
-        vT = b.qkvT[l, pl.ds(2 * DIM + row, HD), :]
-        if l == 0:
-            kn = kT.T
-        else:
-            kn = jnp.concatenate([kT, b.kextra[...]], axis=0).T
-        for c in range(NCH):
+    norm_in(0)
+    norm_in(1)
+    rotate(0)
+    norm_in(2)
+    rotate(1)
+    rotate(2)
+
+    def group(i, carry):
+        heads = [2 * i, 2 * i + 1]
+        rows_of = [pl.multiple_of(h * HD, HD) for h in heads]
+        keys = []
+        for row in rows_of:
+            kT = b.qkvT[l, pl.ds(DIM + row, HD), :]
+            keys.append(kT.T if l == 0 else jnp.concatenate([kT, b.kextra[...]], axis=0).T)
+
+        def score(n):
+            k, c = divmod(n, NCH)
+            k0, k1 = KEYS[l][c]
+            qT = b.qkvT[l, pl.ds(rows_of[k], HD), pl.ds(c * CH, CH)]
+            if l == 0:
+                return nn(keys[k][k0:k1], qT) + b.bias[c, :k1 - k0, :].astype(F32)
+            return nn(keys[k], jnp.concatenate([qT, b.qextra[...]], axis=0))
+
+        total = len(heads) * NCH
+        s = score(0)
+        for n in range(total):
+            k, c = divmod(n, NCH)
             sl = pl.ds(c * CH, CH)
             k0, k1 = KEYS[l][c]
-            qT = b.qkvT[l, pl.ds(row, HD), sl]
-            if l == 0:
-                s = nn(kn[k0:k1], qT) + b.bias[c, :k1 - k0, :].astype(F32)
-            else:
-                s = nn(kn, jnp.concatenate([qT, b.qextra[...]], axis=0))
+            later = score(n + 1) if n + 1 < total else None
             m = jnp.max(s, axis=0, keepdims=True)
             e = jnp.exp(s - m)
             p = (e * (1.0 / jnp.sum(e, axis=0, keepdims=True))).astype(BF16)
             if l == 0:
-                b.p0[h, c, :k1 - k0, :] = p
+                b.p0[heads[k], c, :k1 - k0, :] = p
             else:
-                b.p1[h, :, sl] = p
-            b.oT[l, pl.ds(row, HD), sl] = nn(vT[:, k0:k1], p).astype(BF16)
-
-    def pair(i, carry):
-        head(2 * i)
-        head(2 * i + 1)
+                b.p1[heads[k], :, sl] = p
+            vT = b.qkvT[l, pl.ds(2 * DIM + rows_of[k], HD), k0:k1]
+            b.oT[l, pl.ds(rows_of[k], HD), sl] = nn(vT, p).astype(BF16)
+            s = later
         return carry
-    lax.fori_loop(0, HEADS // 2, pair, 0)
-
-    for c in range(NCH):
+    lax.fori_loop(0, HEADS // 2, group, 0)
+
+    def open_mlp(c):
         sl = pl.ds(c * CH, CH)
         hb = (b.xT[l, :, sl].astype(F32) + nn(b.wTout[l], b.oT[l, :, sl])).astype(BF16)
         b.hT[l, :, sl] = hb
-        u2 = ln_fwd(hb.astype(F32), b.g[1, l], st, 2, sl)
-        mix = nn(b.wTin[l], u2)
-        b.mixT[l, :, sl] = mix
-        act = (gelu_parts(mix[:FFN])[0] * mix[FFN:]).astype(BF16)
-        y = (hb.astype(F32) + nn(b.wTdown[l], act)).astype(BF16)
-        write_y(c, sl, y)
+        b.mixT[l, :, sl] = nn(b.wTin[l], ln_fwd(hb.astype(F32), b.g[1, l], st, 2, sl))
+
+    def close_mlp(c):
+        sl = pl.ds(c * CH, CH)
+        act = (gelu_parts(b.mixT[l, :FFN, sl])[0] * b.mixT[l, FFN:, sl]).astype(BF16)
+        write_y(c, sl, (b.hT[l, :, sl].astype(F32) + nn(b.wTdown[l], act)).astype(BF16))
+
+    open_mlp(0)
+    open_mlp(1)
+    close_mlp(0)
+    open_mlp(2)
+    close_mlp(1)
+    close_mlp(2)
 
 
 def backward(l, b, read_dy, write_dx):
     st = b.st.at[l]
-    for c in range(NCH):
-        sl = pl.ds(c * CH, CH)
-        dy = read_dy(c, sl)
-        dyb = dy.astype(BF16)
+    tmp = {}
+
+    def gate(c):
+        sl = pl.ds(c * CH, CH)
+        dyb = read_dy(c, sl).astype(BF16)
         b.dybT[:, sl] = dyb
-        dact = nn(b.wdown[l], dyb)
+        tmp['act', c] = nn(b.wdown[l], dyb)
+
+    def ungate(c):
+        sl = pl.ds(c * CH, CH)
+        dact = tmp.pop(('act', c))
         a, g = b.mixT[l, :FFN, sl], b.mixT[l, FFN:, sl]
         ge, cdf = gelu_parts(a)
         b.actT[:, sl] = (ge * g).astype(BF16)
         pdf = jnp.exp(a * a * -0.5) * 0.3989422804014327
         b.dbigT[:FFN, sl] = (dact * g * (cdf + a * pdf)).astype(BF16)
         b.dbigT[FFN:, sl] = (dact * ge).astype(BF16)
-        du = nn(b.win[l], b.dbigT[:, sl])
-        dn, dg, b.uT[:, sl] = ln_bwd(b.hT[l, :, sl].astype(F32), du, b.g[1, l], st, 2, sl)
+        tmp['du', c] = nn(b.win[l], b.dbigT[:, sl])
+
+    def unnorm(c):
+        sl = pl.ds(c * CH, CH)
+        dn, dg, b.uT[:, sl] = ln_bwd(b.hT[l, :, sl].astype(F32), tmp.pop(('du', c)), b.g[1, l], st, 2, sl)
         b.dg[1, l] += dg
-        dh = dy + dn
+        dh = read_dy(c, sl) + dn
         b.dyT[:, sl] = dh
         dhb = dh.astype(BF16)
         b.dhbT[:, sl] = dhb
         b.doT[:, sl] = nn(b.wout[l], dhb).astype(BF16)
+
+    gate(0)
+    gate(1)
+    ungate(0)
+    gate(2)
+    ungate(1)
+    unnorm(0)
+    ungate(2)
+    unnorm(1)
     b.adown[l] += nt(b.actT[...], b.dybT[...])
+    unnorm(2)
     b.ain[l] += nt(b.uT[...], b.dbigT[...])
     b.aout[l] += nt(b.oT[l], b.dhbT[...])
 
-    def head(h):
-        row = pl.multiple_of(h * HD, HD)
-        qT = b.qkvT[l, pl.ds(row, HD), :]
-        kT = b.qkvT[l, pl.ds(DIM + row, HD), :]
-        vn = b.qkvT[l, pl.ds(2 * DIM + row, HD), :].T
-        doT = b.doT[pl.ds(row, HD), :]
-        prod = doT.astype(F32) * b.oT[l, pl.ds(row, HD), :].astype(F32)
-        delta = jnp.sum(prod, axis=0, keepdims=True)
-        dq, dk, dv = [], [None] * 6, [None] * 6
-        if l == 1:
-            dvT = nt(doT, b.p1[h])
-        for c in range(NCH):
+    def group(i, carry):
+        heads = [2 * i, 2 * i + 1]
+        info = []
+        for h in heads:
+            row = pl.multiple_of(h * HD, HD)
+            doT = b.doT[pl.ds(row, HD), :]
+            prod = doT.astype(F32) * b.oT[l, pl.ds(row, HD), :].astype(F32)
+            info.append((h, row, b.qkvT[l, pl.ds(row, HD), :], b.qkvT[l, pl.ds(DIM + row, HD), :],
+                         b.qkvT[l, pl.ds(2 * DIM + row, HD), :].T, doT, jnp.sum(prod, axis=0, keepdims=True)))
+
+        def dprob(n):
+            k, c = divmod(n, NCH)
+            k0, k1 = KEYS[l][c]
+            return nn(info[k][4][k0:k1], info[k][5][:, c * CH:(c + 1) * CH])
+
+        cos, sin = b.rope[l, 0], -b.rope[l, 1]
+        total = len(heads) * NCH
+        dp = dprob(0)
+        for n in range(total):
+            k, c = divmod(n, NCH)
+            h, row, qT, kT, _, doT, delta = info[k]
+            if c == 0:
+                dq, dk, dv = [], [None] * 6, [None] * 6
+                if l == 1:
+                    dvT = nt(doT, b.p1[h])
             cs = slice(c * CH, (c + 1) * CH)
             sl = pl.ds(c * CH, CH)
             k0, k1 = KEYS[l][c]
+            later = dprob(n + 1) if n + 1 < total else None
             p = b.p0[h, c, :k1 - k0, :] if l == 0 else b.p1[h, :, sl]
-            dp = nn(vn[k0:k1], doT[:, cs])
             ds = (p.astype(F32) * (dp - delta[:, cs])).astype(BF16)
+            dp = later
             dq.append(nn(kT[:, k0:k1], ds) * 0.125)
             if l == 1:
                 b.p1[h, :, sl] = ds
@@ -194,28 +250,33 @@
                     js = slice(j * 128 - k0, (j + 1) * 128 - k0)
                     dk[j] = dkc[:, js] if dk[j] is None else dk[j] + dkc[:, js]
                     dv[j] = dvc[:, js] if dv[j] is None else dv[j] + dvc[:, js]
-        if l == 1:
-            dkT = nt(qT, b.p1[h])
-        else:
-            dkT, dvT = jnp.concatenate(dk, axis=1), jnp.concatenate(dv, axis=1)
-        dqT = jnp.concatenate(dq, axis=1)
-        cos, sin = b.rope[l, 0], -b.rope[l, 1]
-        b.dbigT[pl.ds(row, HD), :] = turn(dqT, cos, sin).astype(BF16)
-        b.dbigT[pl.ds(DIM + row, HD), :] = turn(dkT, cos, sin).astype(BF16)
-        b.dbigT[pl.ds(2 * DIM + row, HD), :] = dvT.astype(BF16)
-
-    def pair(i, carry):
-        head(2 * i)
-        head(2 * i + 1)
+            if c < NCH - 1:
+                continue
+            if l == 1:
+                dkT = nt(qT, b.p1[h])
+            else:
+                dkT, dvT = jnp.concatenate(dk, axis=1), jnp.concatenate(dv, axis=1)
+            b.dbigT[pl.ds(row, HD), :] = turn(jnp.concatenate(dq, axis=1), cos, sin).astype(BF16)
+            b.dbigT[pl.ds(DIM + row, HD), :] = turn(dkT, cos, sin).astype(BF16)
+            b.dbigT[pl.ds(2 * DIM + row, HD), :] = dvT.astype(BF16)
         return carry
-    lax.fori_loop(0, HEADS // 2, pair, 0)
-
-    for c in range(NCH):
-        sl = pl.ds(c * CH, CH)
-        du = nn(b.wqkv[l], b.dbigT[:, sl])
-        dn, dg, b.uT[:, sl] = ln_bwd(b.xT[l, :, sl].astype(F32), du, b.g[0, l], st, 0, sl)
+    lax.fori_loop(0, HEADS // 2, group, 0)
+
+    def unproject(c):
+        tmp['du', c] = nn(b.wqkv[l], b.dbigT[:, pl.ds(c * CH, CH)])
+
+    def finish(c):
+        sl = pl.ds(c * CH, CH)
+        dn, dg, b.uT[:, sl] = ln_bwd(b.xT[l, :, sl].astype(F32), tmp.pop(('du', c)), b.g[0, l], st, 0, sl)
         b.dg[0, l] += dg
         write_dx(c, sl, b.dyT[:, sl] + dn)
+
+    unproject(0)
+    unproject(1)
+    finish(0)
+    unproject(2)
+    finish(1)
+    finish(2)
     b.aqkv[l] += nt(b.uT[...], b.dbigT[...])
 
 

time: 614 us -> 480 us (0.78)
  Pallas kernels: 593 us -> 459 us
    pallas_call x1, Pallas kernels: 593 us -> 459 us  [run_kernel(): pl.pallas_call(kernel, out_shape=outs, in_specs=[any_spec] * 3 + [vm] * 6...]
where the time goes in v1:
time: 480 us
  Pallas kernels  459 us (96%)
  local copies, waits for them, and re-layouts  19.4 us (4%)
    pallas_call x1, Pallas kernels, run_kernel(): pl.pallas_call(kernel, out_shape=outs, in_specs=[any_spec] * 3 + [vm] * 6...  459 us
    unnamed x17, local copies, waits for them, and re-layouts  17.5 us

profile of v1, /device:TPU:0, one launch (start us, length us, event | category | flops | bytes accessed | tf_op | source)
XLA Modules:
  0.0 479.7 jit_solution(16085529551628389584)
XLA Ops:
  0.6 0.7 maximum_convert_fusion
  1.3 1.1 broadcast_in_dim.2.g_ref
  2.5 458.9 %shard_map.161 = (bf16[32,192,384]{2,1,0:T(8,128)(2,1)}, bf16[32,192,384]{2,1,0:T(8,128)(2,1)}, f32[2,384,1152]{2,1,0:T(8,128)}, f32[2,384,384]{2,1,0:T(8,128)},...) custom-call(bf16[32,192,384]{2,1,0:T(8,128)(2,1)} %x_loc.1, ...), custom_call_target="tpu_custom_call" | custom-call | tf_op jit(solution)/shard_map/pallas_call | solution.py:575
  461.4 0.8 fusion
  462.2 0.6 copy_bitcast_fusion
  462.8 0.0 copy-start
  462.8 5.2 %copy.28 = bf16[32,192,384]{2,1,0:T(8,128)(2,1)} copy(bf16[32,192,384]{2,1,0:T(8,128)(2,1)} %get-tuple-element.34) | data formatting | bytes 9437184
  467.9 0.0 copy-done
  467.9 0.0 copy-start.2
  467.9 2.4 copy.29
  470.3 1.3 copy-done.2
  471.6 0.0 copy-start.4
  471.6 0.0 copy-start.1
  471.6 1.8 copy.30
  473.4 0.3 copy-done.4
  473.7 1.0 copy.31
  474.8 1.0 copy-done.1
  475.7 0.0 copy-start.3
  475.7 1.8 copy.32
  477.5 0.9 copy-done.3
  478.5 1.2 copy.33
Async XLA Ops:
  462.8 5.2 %copy-start = (bf16[32,192,384]{2,1,0:T(8,128)(2,1)S(1)}, bf16[32,192,384]{2,1,0:T(8,128)(2,1)}, u32[]{:S(2)}) copy-start(bf16[32,192,384]{2,1,0:T(8,128)(2,1)} %get-tuple-element.35) | copy-start | bytes 14155780
  467.9 3.7 copy-start.2
  471.6 2.1 copy-start.4
  471.6 4.1 copy-start.1
  475.7 2.8 copy-start.3

commit v2 on v1

--- a/solution.py
+++ b/solution.py
@@ -111,7 +111,7 @@
     rotate(2)
 
     def group(i, carry):
-        heads = [2 * i, 2 * i + 1]
+        heads = [3 * i, 3 * i + 1, 3 * i + 2]
         rows_of = [pl.multiple_of(h * HD, HD) for h in heads]
         keys = []
         for row in rows_of:
@@ -144,7 +144,7 @@
             b.oT[l, pl.ds(rows_of[k], HD), sl] = nn(vT, p).astype(BF16)
             s = later
         return carry
-    lax.fori_loop(0, HEADS // 2, group, 0)
+    lax.fori_loop(0, HEADS // 3, group, 0)
 
     def open_mlp(c):
         sl = pl.ds(c * CH, CH)
@@ -210,7 +210,7 @@
     b.aout[l] += nt(b.oT[l], b.dhbT[...])
 
     def group(i, carry):
-        heads = [2 * i, 2 * i + 1]
+        heads = [3 * i, 3 * i + 1, 3 * i + 2]
         info = []
         for h in heads:
             row = pl.multiple_of(h * HD, HD)
@@ -232,8 +232,6 @@
             h, row, qT, kT, _, doT, delta = info[k]
             if c == 0:
                 dq, dk, dv = [], [None] * 6, [None] * 6
-                if l == 1:
-                    dvT = nt(doT, b.p1[h])
             cs = slice(c * CH, (c + 1) * CH)
             sl = pl.ds(c * CH, CH)
             k0, k1 = KEYS[l][c]
@@ -242,25 +240,19 @@
             ds = (p.astype(F32) * (dp - delta[:, cs])).astype(BF16)
             dp = later
             dq.append(nn(kT[:, k0:k1], ds) * 0.125)
-            if l == 1:
-                b.p1[h, :, sl] = ds
-            else:
-                dkc, dvc = nt(qT[:, cs], ds), nt(doT[:, cs], p)
-                for j in range(k0 // 128, k1 // 128):
-                    js = slice(j * 128 - k0, (j + 1) * 128 - k0)
-                    dk[j] = dkc[:, js] if dk[j] is None else dk[j] + dkc[:, js]
-                    dv[j] = dvc[:, js] if dv[j] is None else dv[j] + dvc[:, js]
+            dkc, dvc = nt(qT[:, cs], ds), nt(doT[:, cs], p)
+            for j in range(k0 // 128, k1 // 128):
+                js = slice(j * 128 - k0, (j + 1) * 128 - k0)
+                dk[j] = dkc[:, js] if dk[j] is None else dk[j] + dkc[:, js]
+                dv[j] = dvc[:, js] if dv[j] is None else dv[j] + dvc[:, js]
             if c < NCH - 1:
                 continue
-            if l == 1:
-                dkT = nt(qT, b.p1[h])
-            else:
-                dkT, dvT = jnp.concatenate(dk, axis=1), jnp.concatenate(dv, axis=1)
+            dkT, dvT = jnp.concatenate(dk, axis=1), jnp.concatenate(dv, axis=1)
             b.dbigT[pl.ds(row, HD), :] = turn(jnp.concatenate(dq, axis=1), cos, sin).astype(BF16)
             b.dbigT[pl.ds(DIM + row, HD), :] = turn(dkT, cos, sin).astype(BF16)
             b.dbigT[pl.ds(2 * DIM + row, HD), :] = dvT.astype(BF16)
         return carry
-    lax.fori_loop(0, HEADS // 2, group, 0)
+    lax.fori_loop(0, HEADS // 3, group, 0)
 
     def unproject(c):
         tmp['du', c] = nn(b.wqkv[l], b.dbigT[:, pl.ds(c * CH, CH)])

time: 480 us -> 467 us (0.973)
  Pallas kernels: 459 us -> 446 us
    pallas_call x1, Pallas kernels: 459 us -> 446 us  [run_kernel(): pl.pallas_call(kernel, out_shape=outs, in_specs=[any_spec] * 3 + [vm] * 6...]
where the time goes in v2:
time: 467 us
  Pallas kernels  446 us (96%)
  local copies, waits for them, and re-layouts  19.4 us (4%)
    pallas_call x1, Pallas kernels, run_kernel(): pl.pallas_call(kernel, out_shape=outs, in_specs=[any_spec] * 3 + [vm] * 6...  446 us
    unnamed x17, local copies, waits for them, and re-layouts  17.5 us

profile of v2, /device:TPU:0, one launch (start us, length us, event | category | flops | bytes accessed | tf_op | source)
XLA Modules:
  0.0 467.1 jit_solution(7541555592838014371)
XLA Ops:
  0.6 0.7 maximum_convert_fusion
  1.3 1.1 broadcast_in_dim.2.g_ref
  2.5 446.3 %shard_map.161 = (bf16[32,192,384]{2,1,0:T(8,128)(2,1)}, bf16[32,192,384]{2,1,0:T(8,128)(2,1)}, f32[2,384,1152]{2,1,0:T(8,128)}, f32[2,384,384]{2,1,0:T(8,128)},...) custom-call(bf16[32,192,384]{2,1,0:T(8,128)(2,1)} %x_loc.1, ...), custom_call_target="tpu_custom_call" | custom-call | tf_op jit(solution)/shard_map/pallas_call | solution.py:567
  448.8 0.8 fusion
  449.6 0.6 copy_bitcast_fusion
  450.2 0.0 copy-start
  450.2 5.2 %copy.28 = bf16[32,192,384]{2,1,0:T(8,128)(2,1)} copy(bf16[32,192,384]{2,1,0:T(8,128)(2,1)} %get-tuple-element.34) | data formatting | bytes 9437184
  455.4 0.0 copy-done
  455.4 0.0 copy-start.2
  455.4 2.4 copy.29
  457.8 1.3 copy-done.2
  459.1 0.0 copy-start.4
  459.1 0.0 copy-start.1
  459.1 1.8 copy.30
  460.9 0.3 copy-done.4
  461.2 1.0 copy.31
  462.2 1.0 copy-done.1
  463.1 0.0 copy-start.3
  463.1 1.8 copy.32
  464.9 0.9 copy-done.3
  465.9 1.2 copy.33
Async XLA Ops:
  450.2 5.2 %copy-start = (bf16[32,192,384]{2,1,0:T(8,128)(2,1)S(1)}, bf16[32,192,384]{2,1,0:T(8,128)(2,1)}, u32[]{:S(2)}) copy-start(bf16[32,192,384]{2,1,0:T(8,128)(2,1)} %get-tuple-element.35) | copy-start | bytes 14155780
  455.4 3.7 copy-start.2
  459.1 2.1 copy-start.4
  459.1 4.1 copy-start.1
  463.1 2.8 copy-start.3
